TPU v7x, 32 devices: a whole 2x2x4 slice. The times are simulated.
32 devices in a mesh: section: 8 (over y, x, core), tensor: 4 (over z).
Axes of the slice: x: 2, y: 2, z: 4, core: 2. Of those that a mesh axis runs over, the one named last changes fastest.
Arguments:
- section_inputs: bfloat16 [8, 512, 1024], P('section', 'tensor'), may hold values from -6 to 6
- w_in: bfloat16 [8, 2304, 1024], P('section', 'tensor'), may hold values from -0.1875 to 0.1875
- in_bias: bfloat16 [8, 2304], P('section', 'tensor'), may hold values from -3 to 3
- w_out: bfloat16 [8, 2304, 1024], P('section', 'tensor'), may hold values from -0.125 to 0.125
- out_bias: float32 [8, 1024], P('section'), may hold values from -2 to 2
- norm_gain: float32 [8, 1024], P('section'), may hold values from 0.1 to 1.9
- norm_bias: float32 [8, 1024], P('section'), may hold values from -2 to 2
- patches: bfloat16 [8, 512, 1024], P(None, 'tensor'), may hold values from -6 to 6
- plan: int32 [3], replicated, may hold values from 0 to 7, as said below
Outputs:
- received: bfloat16 [8, 4, 512, 1024], P('section', None, 'tensor')
Inputs may be any that keep to these rules, and one draw needn't show every extreme that they name: `plan`: the first min(8, 3) entries are all different.
All inputs are finite; a program needn't handle non-finite values.
Results may differ from a plain program's by a relative error of at most 0.0065.
Values may be sent and summed in bfloat16 or wider, within the bound.
A program may use at most 64 MiB of HBM per device.

v0:
```python
import jax
import jax.numpy as jnp
from jax import lax
from jax.sharding import PartitionSpec as P

TICKS = 4


norm_floor = 0.1
gelu_slope = 1.702


def passed_along(value, axis, steps):
    count = lax.axis_size(axis)
    pairs = [(source, (source + steps) % count) for source in range(count)]
    return lax.ppermute(value, axis, pairs)


def normalize(current, gain_row, shift_row):
    widened = current.astype(jnp.float32)
    average = jnp.mean(widened, axis=-1, keepdims=True)
    centered = widened - average
    variance = jnp.mean(centered * centered, axis=-1, keepdims=True)
    normed = (centered * lax.rsqrt(variance + norm_floor) * gain_row + shift_row).astype(
        jnp.bfloat16
    )
    return (normed, widened)


def activate(preact):
    return preact * jax.nn.sigmoid(gelu_slope * preact)


def hidden_units(normed, rows_in, rows_bias):
    preact = lax.dot_general(
        normed, rows_in, (((1,), (1,)), ((), ())), preferred_element_type=jnp.float32
    )
    return activate(preact + rows_bias.astype(jnp.float32)).astype(jnp.bfloat16)


def apply_block(current, gain_row, shift_row, full_in, full_bias, full_out, bias_row):
    normed, widened = normalize(current, gain_row, shift_row)
    hidden = hidden_units(normed, full_in, full_bias)
    return (
        widened + jnp.dot(hidden, full_out, preferred_element_type=jnp.float32) + bias_row
    ).astype(jnp.bfloat16)


def shards(section_inputs, w_in, in_bias, w_out, out_bias, norm_gain, norm_bias, patches, plan):
    current = section_inputs[0]
    gain_row = norm_gain[0]
    shift_row = norm_bias[0]
    bias_row = out_bias[0]
    section_index = lax.axis_index("section")
    full_in, full_bias, full_out = (
        lax.all_gather(w_in[0], "tensor", axis=0, tiled=True),
        lax.all_gather(in_bias[0], "tensor", axis=0, tiled=True),
        lax.all_gather(w_out[0], "tensor", axis=0, tiled=True),
    )
    produced = apply_block(current, gain_row, shift_row, full_in, full_bias, full_out, bias_row)
    records = []
    for tick_index in range(TICKS):
        if tick_index > 0:
            produced = apply_block(
                current, gain_row, shift_row, full_in, full_bias, full_out, bias_row
            )
        arrived = passed_along(produced, "section", 1)
        records.append(arrived)
        if tick_index + 1 < TICKS:
            selected = lax.dynamic_index_in_dim(patches, plan[tick_index], 0, keepdims=False)
            current = jnp.where(section_index == 0, selected, arrived)
    return jnp.stack(records, axis=0)[None]


def solution(mesh):
    placed = (
        P("section", "tensor", None),
        P("section", "tensor", None),
        P("section", "tensor"),
        P("section", "tensor", None),
        P("section", None),
        P("section", None),
        P("section", None),
        P(None, "tensor", None),
        P(),
    )
    return jax.shard_map(
        shards,
        mesh=mesh,
        in_specs=placed,
        out_specs=P("section", None, "tensor", None),
        check_vma=False,
    )
```

profile of v0, /device:TPU:0, one launch (start us, length us, event | category | flops | bytes accessed | tf_op | source)
XLA Modules:
  0.0 254.6 jit_solution(12723536823226254353)
XLA Ops:
  6.5 0.0 copy-start.6
  6.5 0.0 copy-start.2
  6.5 0.0 copy-start
  6.5 0.0 all-gather.6.cloned.1.call-start
  6.5 0.7 all-gather.6.cloned.1.call-update
  7.3 0.0 copy-start.3
  7.3 0.0 copy-start.4
  7.3 0.0 copy-start.5
  7.3 0.0 all-gather.8.cloned.1.call-start
  7.3 0.7 all-gather.8.cloned.1.call-update
  8.1 0.0 copy-done.6
  8.1 0.6 dynamic-slice
  9.3 0.0 copy-done.2
  9.3 0.2 dynamic-update-slice
  9.6 13.8 %all-reduce = bf16[2304]{0:T(1024)(128)(2,1)S(1)} all-reduce(bf16[2304]{0:T(1024)(128)(2,1)S(1)} %dynamic-update-slice), channel_id=3, replica_groups=mesh['section'=8,'tensor'=4] {'tensor'}, use_global_device_ids=true, to_apply=%add | all-reduce | flops 2304 | bytes 9216
  23.4 0.0 copy-done
  23.4 0.1 convert_reduce_fusion.3
  23.6 0.2 fusion.113
  23.8 77.3 %all-gather.6.cloned.1.call-done = bf16[1,2304,1024]{2,1,0:T(8,128)(2,1)} async-done(((bf16[1,576,1024]{2,1,0:T(8,128)(2,1)}), bf16[1,2304,1024]{2,1,0:T(8,128)(2,1)}) %all-gather.6.cloned.1.call-update) | async-done | bytes 4718608 | tf_op jit(solution)/shard_map/all_gather | solution.py:56
  101.0 89.4 %all-gather.8.cloned.1.call-done = bf16[1,2304,1024]{2,1,0:T(8,128)(2,1)} async-done(((bf16[1,576,1024]{2,1,0:T(8,128)(2,1)}), bf16[1,2304,1024]{2,1,0:T(8,128)(2,1)}) %all-gather.8.cloned.1.call-update) | async-done | bytes 4718608 | tf_op jit(solution)/shard_map/all_gather | solution.py:58
  190.4 0.0 copy-done.3
  190.5 0.0 copy-done.4
  190.5 0.0 copy-done.5
  190.5 0.0 copy-start.1
  190.5 6.3 %fusion.52 = bf16[128,1024]{1,0:T(8,128)(2,1)S(1)} fusion(bf16[1,2304,1024]{2,1,0:T(8,128)(2,1)} %all-gather.8.cloned.1.call-done, bf16[1,2304,1024]{2,1,0:T(8,128)(2,1)} %all-gather.6.cloned.1.call-done, bf16[1,128,1024]{2,1,0:T(8,128)(2,1)S(1)} %copy-done, f32[2304]{0:T(1024)S(1)} %convert_element_type.76, f32[1024]{0:T(1024)S(1)} %bitcast.112, ...), kind=kOutput, calls=%fused_computation.28 | convolution fusion | flops 1211334656 | bytes 9984000 | tf_op jit(solution)/shard_map/dot_general | solution.py:45
  196.7 0.1 collective-permute-start
  196.8 0.0 copy-done.1
  196.8 0.7 fusion.165
  199.4 4.1 %collective-permute-done = bf16[128,1024]{1,0:T(8,128)(2,1)S(1)} collective-permute-done((bf16[128,1024]{1,0:T(8,128)(2,1)S(1)}, bf16[128,1024]{1,0:T(8,128)(2,1)S(1)}, u32[]{:S(2)}, u32[]{:S(2)}) %collective-permute-start) | collective-permute-done | bytes 262176 | tf_op jit(solution)/shard_map/ppermute | solution.py:16
  203.5 1.1 convert_reduce_fusion.2
  204.6 0.2 fusion.109
  204.8 6.3 %fusion.55 = bf16[128,1024]{1,0:T(8,128)(2,1)S(1)} fusion(bf16[1,2304,1024]{2,1,0:T(8,128)(2,1)} %all-gather.8.cloned.1.call-done, bf16[128,1024]{1,0:T(8,128)(2,1)S(1)} %get-tuple-element.10, bf16[1,2304,1024]{2,1,0:T(8,128)(2,1)} %all-gather.6.cloned.1.call-done, f32[2304]{0:T(1024)S(1)} %convert_element_type.76, f32[128]{0:T(128)S(1)} %add_rsqrt_fusion.2, ...), kind=kOutput, calls=%fused_computation.29 | convolution fusion | flops 1211334656 | bytes 9984000 | tf_op jit(solution)/shard_map/dot_general | solution.py:45
  211.1 0.1 collective-permute-start.1
  213.2 4.7 %collective-permute-done.1 = bf16[128,1024]{1,0:T(8,128)(2,1)S(1)} collective-permute-done((bf16[128,1024]{1,0:T(8,128)(2,1)S(1)}, bf16[128,1024]{1,0:T(8,128)(2,1)S(1)}, u32[]{:S(2)}, u32[]{:S(2)}) %collective-permute-start.1) | collective-permute-done | bytes 262176 | tf_op jit(solution)/shard_map/ppermute | solution.py:16
  217.9 1.1 convert_reduce_fusion.1
  219.0 0.2 fusion.105
  219.2 6.3 %fusion.58 = bf16[128,1024]{1,0:T(8,128)(2,1)S(1)} fusion(bf16[1,2304,1024]{2,1,0:T(8,128)(2,1)} %all-gather.8.cloned.1.call-done, bf16[128,1024]{1,0:T(8,128)(2,1)S(1)} %get-tuple-element.8, bf16[1,2304,1024]{2,1,0:T(8,128)(2,1)} %all-gather.6.cloned.1.call-done, f32[2304]{0:T(1024)S(1)} %convert_element_type.76, f32[128]{0:T(128)S(1)} %add_rsqrt_fusion.1, ...), kind=kOutput, calls=%fused_computation.30 | convolution fusion | flops 1211334656 | bytes 9984000 | tf_op jit(solution)/shard_map/dot_general | solution.py:45
  225.5 0.1 collective-permute-start.2
  227.5 4.7 %collective-permute-done.2 = bf16[128,1024]{1,0:T(8,128)(2,1)S(1)} collective-permute-done((bf16[128,1024]{1,0:T(8,128)(2,1)S(1)}, bf16[128,1024]{1,0:T(8,128)(2,1)S(1)}, u32[]{:S(2)}, u32[]{:S(2)}) %collective-permute-start.2) | collective-permute-done | bytes 262176 | tf_op jit(solution)/shard_map/ppermute | solution.py:16
  232.2 1.1 convert_reduce_fusion
  233.4 0.2 fusion.101
  233.6 6.3 %fusion.61 = bf16[128,1024]{1,0:T(8,128)(2,1)S(1)} fusion(bf16[1,2304,1024]{2,1,0:T(8,128)(2,1)} %all-gather.8.cloned.1.call-done, bf16[128,1024]{1,0:T(8,128)(2,1)S(1)} %get-tuple-element.6, bf16[1,2304,1024]{2,1,0:T(8,128)(2,1)} %all-gather.6.cloned.1.call-done, f32[2304]{0:T(1024)S(1)} %convert_element_type.76, f32[128]{0:T(128)S(1)} %add_rsqrt_fusion, ...), kind=kOutput, calls=%fused_computation.31 | convolution fusion | flops 1211334656 | bytes 9984000 | tf_op jit(solution)/shard_map/dot_general | solution.py:45
  239.9 0.1 collective-permute-start.3
  239.9 6.7 %collective-permute-done.3 = bf16[128,1024]{1,0:T(8,128)(2,1)S(1)} collective-permute-done((bf16[128,1024]{1,0:T(8,128)(2,1)S(1)}, bf16[128,1024]{1,0:T(8,128)(2,1)S(1)}, u32[]{:S(2)}, u32[]{:S(2)}) %collective-permute-start.3) | collective-permute-done | bytes 262176 | tf_op jit(solution)/shard_map/ppermute | solution.py:16
  246.6 1.1 maximum_bitcast_fusion
  (11 shorter events, 0.1 us)
Async XLA Ops:
  6.5 1.5 copy-start.6
  6.5 2.8 %copy-start.2 = (bf16[1,576]{1,0:T(2,128)(2,1)S(1)}, bf16[1,576]{1,0:T(2,128)(2,1)}, u32[]{:S(2)}) copy-start(bf16[1,576]{1,0:T(2,128)(2,1)} %param.11) | copy-start | bytes 3460
  6.5 16.9 %copy-start = (bf16[1,128,1024]{2,1,0:T(8,128)(2,1)S(1)}, bf16[1,128,1024]{2,1,0:T(8,128)(2,1)}, u32[]{:S(2)}) copy-start(bf16[1,128,1024]{2,1,0:T(8,128)(2,1)} %param.9) | copy-start | bytes 786436
  6.5 94.5 %all-gather.6.cloned.1.call-start = ((), (), s32[]{:S(2)}) async-start(), calls=%async_computation | async-start | bytes 5898240 | tf_op jit(solution)/shard_map/all_gather | solution.py:56
  7.3 183.2 %copy-start.3 = (f32[1,1024]{1,0:T(1,128)S(1)}, f32[1,1024]{1,0:T(1,128)}, u32[]{:S(2)}) copy-start(f32[1,1024]{1,0:T(1,128)} %param.13) | copy-start | bytes 12292
  7.3 183.2 %copy-start.4 = (f32[1,1024]{1,0:T(1,128)S(1)}, f32[1,1024]{1,0:T(1,128)}, u32[]{:S(2)}) copy-start(f32[1,1024]{1,0:T(1,128)} %param.15) | copy-start | bytes 12292
  7.3 183.2 %copy-start.5 = (f32[1,1024]{1,0:T(1,128)S(1)}, f32[1,1024]{1,0:T(1,128)}, u32[]{:S(2)}) copy-start(f32[1,1024]{1,0:T(1,128)} %param.14) | copy-start | bytes 12292
  7.3 183.2 %all-gather.8.cloned.1.call-start = ((), (), s32[]{:S(2)}) async-start(), calls=%async_computation.1 | async-start | bytes 5898240 | tf_op jit(solution)/shard_map/all_gather | solution.py:58
  190.5 6.4 %copy-start.1 = (s32[3]{0:T(128)S(1)}, s32[3]{0:T(128)}, u32[]{:S(2)}) copy-start(s32[3]{0:T(128)} %param.17) | copy-start | bytes 40
  196.7 6.7 %collective-permute-start = (bf16[128,1024]{1,0:T(8,128)(2,1)S(1)}, bf16[128,1024]{1,0:T(8,128)(2,1)S(1)}, u32[]{:S(2)}, u32[]{:S(2)}) collective-permute-start(bf16[128,1024]{1,0:T(8,128)(2,1)S(1)} %fusion.52), channel_id=1, source_target_pairs={{0,4},{4,8},{8,12},{12,16},{16,20},{20,24},{24,28},{28,0},{1,5},{5... | collective-permute-start | bytes 786440 | tf_op jit(solution)/shard_map/ppermute | solution.py:16
  211.1 6.7 %collective-permute-start.1 = (bf16[128,1024]{1,0:T(8,128)(2,1)S(1)}, bf16[128,1024]{1,0:T(8,128)(2,1)S(1)}, u32[]{:S(2)}, u32[]{:S(2)}) collective-permute-start(bf16[128,1024]{1,0:T(8,128)(2,1)S(1)} %fusion.55), channel_id=1, source_target_pairs={{0,4},{4,8},{8,12},{12,16},{16,20},{20,24},{24,28},{28,0},{1,5},{5... | collective-permute-start | bytes 786440 | tf_op jit(solution)/shard_map/ppermute | solution.py:16
  225.5 6.7 %collective-permute-start.2 = (bf16[128,1024]{1,0:T(8,128)(2,1)S(1)}, bf16[128,1024]{1,0:T(8,128)(2,1)S(1)}, u32[]{:S(2)}, u32[]{:S(2)}) collective-permute-start(bf16[128,1024]{1,0:T(8,128)(2,1)S(1)} %fusion.58), channel_id=1, source_target_pairs={{0,4},{4,8},{8,12},{12,16},{16,20},{20,24},{24,28},{28,0},{1,5},{5... | collective-permute-start | bytes 786440 | tf_op jit(solution)/shard_map/ppermute | solution.py:16
  239.9 6.7 %collective-permute-start.3 = (bf16[128,1024]{1,0:T(8,128)(2,1)S(1)}, bf16[128,1024]{1,0:T(8,128)(2,1)S(1)}, u32[]{:S(2)}, u32[]{:S(2)}) collective-permute-start(bf16[128,1024]{1,0:T(8,128)(2,1)S(1)} %fusion.61), channel_id=1, source_target_pairs={{0,4},{4,8},{8,12},{12,16},{16,20},{20,24},{24,28},{28,0},{1,5},{5... | collective-permute-start | bytes 786440 | tf_op jit(solution)/shard_map/ppermute | solution.py:16
Sparse Core Ops, SparseCore 0:
  8.9 92.0 all-gather.5
  102.6 87.7 all-gather.7
where the time goes:
time: 255 us
  waiting for transfers between devices  188 us (74%)
  matrix products  25.1 us (10%)
  between operations  20.1 us (8%)
  blocking collectives  13.8 us (5%)
  other arithmetic  5.5 us (2%)
    all_gather x1, waiting for transfers between devices, shards(): lax.all_gather(w_out[0], 'tensor', axis=0, tiled=True)  89.4 us
    all_gather x1, waiting for transfers between devices, shards(): lax.all_gather(w_in[0], 'tensor', axis=0, tiled=True)  77.3 us
    dot_general x4, matrix products, apply_block(): jnp.dot(hidden, full_out, preferred_element_type=jnp.float32)  25.1 us
    ppermute x4, waiting for transfers between devices, passed_along(): return lax.ppermute(value, axis, pairs)  20.2 us
    unnamed x1, blocking collectives  13.8 us
  transfers between devices with their start and end apart: 6, of which 6 were waited for; matrix products, arithmetic and copies ran while one was open for 1% of the time, Pallas kernels for 0%

commit v1 on v0

v1 whole, which is shorter than its diff:
```python
import functools

import jax
import jax.numpy as jnp
from jax import lax
from jax.experimental import pallas as pl
from jax.experimental.pallas import tpu as pltpu
from jax.sharding import PartitionSpec as P

TICKS = 4
CHUNKS = 4
VMEM_BYTES = 60 * 1024 * 1024

norm_floor = 0.1
gelu_slope = 1.702
MESH = pl.DeviceIdType.MESH


def activate(preact):
    return preact * jax.nn.sigmoid(gelu_slope * preact)


def normalize(widened, gain_row, shift_row):
    average = jnp.mean(widened, axis=-1, keepdims=True)
    centered = widened - average
    variance = jnp.mean(centered * centered, axis=-1, keepdims=True)
    return (centered * lax.rsqrt(variance + norm_floor) * gain_row + shift_row).astype(
        jnp.bfloat16
    )


def relay_kernel(
    n, sections, chunks,
    x_ref, win_ref, ib_ref, wout_ref, ob_ref, gain_ref, shift_ref, patches_ref, plan_ref,
    o_ref,
    gathered, part, right_out, right_in, left_out, left_in, own, produced, arrived,
    ag_send, ag_recv, rs_send, rs_recv, hop_send, hop_recv,
):
    items = TICKS * chunks
    rows, width = x_ref.shape[1], x_ref.shape[2]
    me = lax.axis_index("tensor")
    section = lax.axis_index("section")
    following = lax.rem(section + 1, sections)
    preceding = lax.rem(section + sections - 1, sections)
    has_left, has_right = me > 0, me < n - 1

    barrier = pltpu.get_barrier_semaphore()

    def greet(tensor, sect):
        pl.semaphore_signal(
            barrier, inc=1, device_id={"section": sect, "tensor": tensor}, device_id_type=MESH
        )

    greet(me, following)
    greet(me, preceding)
    pl.when(has_left)(lambda: greet(me - 1, section))
    pl.when(has_right)(lambda: greet(me + 1, section))
    pl.semaphore_wait(barrier, 2 + has_left.astype(jnp.int32) + has_right.astype(jnp.int32))

    def gather_copy(item, shard, way):
        return pltpu.make_async_remote_copy(
            src_ref=gathered.at[item, shard],
            dst_ref=gathered.at[item, shard],
            send_sem=ag_send.at[way, item, shard],
            recv_sem=ag_recv.at[way, item, shard],
            device_id={"section": section, "tensor": me + 1 if way == 0 else me - 1},
            device_id_type=MESH,
        )

    def reduce_copy(item, dest, way):
        return pltpu.make_async_remote_copy(
            src_ref=(right_out if way == 0 else left_out).at[item, dest],
            dst_ref=(right_in if way == 0 else left_in).at[item, dest],
            send_sem=rs_send.at[way, item, dest],
            recv_sem=rs_recv.at[way, item, dest],
            device_id={"section": section, "tensor": me + 1 if way == 0 else me - 1},
            device_id_type=MESH,
        )

    def relay_copy(item):
        return pltpu.make_async_remote_copy(
            src_ref=produced.at[item],
            dst_ref=arrived.at[item],
            send_sem=hop_send.at[item],
            recv_sem=hop_recv.at[item],
            device_id={"section": following, "tensor": me},
            device_id_type=MESH,
        )

    def begin(item):
        @pl.when(item < chunks)
        def _():
            own[item] = x_ref[item]

        @pl.when(item >= chunks)
        def _():
            before = item - chunks
            relay_copy(before).wait_recv()
            value = arrived[before]
            o_ref[before] = value
            own[item] = value

            @pl.when(section == 0)
            def _():
                entry = plan_ref[lax.div(before, chunks)]
                own[item] = patches_ref[entry, lax.rem(before, chunks)]

        gathered[item, me] = normalize(
            own[item].astype(jnp.float32), gain_ref[...], shift_ref[...]
        )
        pl.when(has_right)(lambda: gather_copy(item, me, 0).start())
        pl.when(has_left)(lambda: gather_copy(item, me, 1).start())

    def pass_on(item, hop):
        @pl.when(me >= hop)
        def _():
            gather_copy(item, me - hop, 0).wait_recv()
            pl.when(has_right)(lambda: gather_copy(item, me - hop, 0).start())

        @pl.when(me + hop < n)
        def _():
            gather_copy(item, me + hop, 1).wait_recv()
            pl.when(has_left)(lambda: gather_copy(item, me + hop, 1).start())

    def multiply(item):
        slot = lax.rem(item, 4)
        tokens = gathered[item].reshape(n * rows, width)
        preact = lax.dot_general(
            tokens, win_ref[...], (((1,), (1,)), ((), ())), preferred_element_type=jnp.float32
        )
        hidden = activate(preact + ib_ref[...].astype(jnp.float32)).astype(jnp.bfloat16)
        part[slot] = jnp.dot(
            hidden, wout_ref[...], preferred_element_type=jnp.float32
        ).reshape(n, rows, width)

    def reduce_step(item, hop):
        slot = lax.rem(item, 4)

        @pl.when(me == hop)
        def _():
            for dest in range(n - 1, hop - 1, -1):
                if hop > 0:
                    reduce_copy(item, dest, 0).wait_recv()
                    value = part[slot, dest] + right_in[item, dest].astype(jnp.float32)
                else:
                    value = part[slot, dest]
                if dest > hop:
                    right_out[item, dest] = value.astype(jnp.bfloat16)
                    reduce_copy(item, dest, 0).start()
                elif hop > 0:
                    part[slot, dest] = value

        mine = n - 1 - hop

        @pl.when(me == mine)
        def _():
            for dest in range(0, mine + 1):
                if hop > 0:
                    reduce_copy(item, dest, 1).wait_recv()
                    value = part[slot, dest] + left_in[item, dest].astype(jnp.float32)
                else:
                    value = part[slot, dest]
                if dest < mine:
                    left_out[item, dest] = value.astype(jnp.bfloat16)
                    reduce_copy(item, dest, 1).start()
                elif hop > 0:
                    part[slot, dest] = value

    def finish(item):
        slot = lax.rem(item, 4)
        produced[item] = (
            own[item].astype(jnp.float32) + part[slot, me] + ob_ref[...]
        ).astype(jnp.bfloat16)
        relay_copy(item).start()

    def stage(number, item):
        if number == 0:
            begin(item)
        elif number < n:
            pass_on(item, number)
        if number == n - 1:
            multiply(item)
        if number >= n - 1:
            reduce_step(item, number - (n - 1))
        if number == 2 * n - 2:
            finish(item)

    def turn(step, carry):
        for parity in range(2):
            for number in range(2 * n - 2, -1, -1):
                if number % 2 == parity:
                    item = step - number // 2
                    pl.when((item >= 0) & (item < items))(
                        functools.partial(stage, number, item)
                    )
        return carry

    lax.fori_loop(0, items + n - 1, turn, 0)

    def drain(item, carry):
        relay_copy(item).wait_send()

        @pl.when(item >= items - chunks)
        def _():
            relay_copy(item).wait_recv()
            o_ref[item] = arrived[item]

        for other in range(n):
            pl.when(has_right & (me >= other))(
                lambda: gather_copy(item, other, 0).wait_send()
            )
            pl.when(has_left & (me <= other))(
                lambda: gather_copy(item, other, 1).wait_send()
            )
            pl.when(me < other)(lambda: reduce_copy(item, other, 0).wait_send())
            pl.when(me > other)(lambda: reduce_copy(item, other, 1).wait_send())
        return carry

    lax.fori_loop(0, items, drain, 0)


def relay_call(n, sections, chunks, args):
    x, w_in, in_bias, w_out, out_bias, gain, shift, patches, plan = args
    tokens, width = x.shape
    rows = tokens // chunks
    items = TICKS * chunks
    micro = patches.shape[0]
    bf16 = jnp.bfloat16
    vmem = pl.BlockSpec(memory_space=pltpu.VMEM)
    every = (items, n, rows, width)
    dma = pltpu.SemaphoreType.DMA
    out = pl.pallas_call(
        functools.partial(relay_kernel, n, sections, chunks),
        out_shape=jax.ShapeDtypeStruct((items, rows, width), bf16),
        in_specs=[vmem] * 8 + [pl.BlockSpec(memory_space=pltpu.SMEM)],
        out_specs=vmem,
        scratch_shapes=[
            pltpu.VMEM(every, bf16),
            pltpu.VMEM((4, n, rows, width), jnp.float32),
            pltpu.VMEM(every, bf16),
            pltpu.VMEM(every, bf16),
            pltpu.VMEM(every, bf16),
            pltpu.VMEM(every, bf16),
            pltpu.VMEM((items, rows, width), bf16),
            pltpu.VMEM((items, rows, width), bf16),
            pltpu.VMEM((items, rows, width), bf16),
            dma((2, items, n)),
            dma((2, items, n)),
            dma((2, items, n)),
            dma((2, items, n)),
            dma((items,)),
            dma((items,)),
        ],
        compiler_params=pltpu.CompilerParams(
            collective_id=0, has_side_effects=True, vmem_limit_bytes=VMEM_BYTES
        ),
    )(
        x.reshape(chunks, rows, width),
        w_in,
        in_bias.reshape(1, -1),
        w_out,
        out_bias.reshape(1, -1),
        gain.reshape(1, -1),
        shift.reshape(1, -1),
        patches.reshape(micro, chunks, rows, width),
        plan,
    )
    return out.reshape(1, TICKS, tokens, width)


def passed_along(value, axis, steps):
    count = lax.axis_size(axis)
    pairs = [(source, (source + steps) % count) for source in range(count)]
    return lax.ppermute(value, axis, pairs)


def gathered_weights(args):
    current, w_in, in_bias, w_out, bias_row, gain_row, shift_row, patches, plan = args
    section_index = lax.axis_index("section")
    full_in, full_bias, full_out = (
        lax.all_gather(value, "tensor", axis=0, tiled=True) for value in (w_in, in_bias, w_out)
    )
    records = []
    for tick_index in range(TICKS):
        widened = current.astype(jnp.float32)
        normed = normalize(widened, gain_row, shift_row)
        preact = lax.dot_general(
            normed, full_in, (((1,), (1,)), ((), ())), preferred_element_type=jnp.float32
        )
        hidden = activate(preact + full_bias.astype(jnp.float32)).astype(jnp.bfloat16)
        produced = (
            widened + jnp.dot(hidden, full_out, preferred_element_type=jnp.float32) + bias_row
        ).astype(jnp.bfloat16)
        arrived = passed_along(produced, "section", 1)
        records.append(arrived)
        if tick_index + 1 < TICKS:
            selected = lax.dynamic_index_in_dim(patches, plan[tick_index], 0, keepdims=False)
            current = jnp.where(section_index == 0, selected, arrived)
    return jnp.stack(records, axis=0)[None]


def shards(n, sections, *blocks):
    args = tuple(block[0] for block in blocks[:7]) + blocks[7:]
    tokens, width = args[0].shape
    held = 2 * width * (
        TICKS * tokens * (5 * n + 4) + 2 * args[1].shape[0] + tokens * (1 + args[7].shape[0])
    ) + 16 * n * tokens * width // CHUNKS
    if tokens % (CHUNKS * 16) or n < 2 or sections < 2 or held > VMEM_BYTES * 3 // 4:
        return gathered_weights(args)
    return relay_call(n, sections, CHUNKS, args)


def solution(mesh):
    placed = (
        P("section", "tensor", None),
        P("section", "tensor", None),
        P("section", "tensor"),
        P("section", "tensor", None),
        P("section", None),
        P("section", None),
        P("section", None),
        P(None, "tensor", None),
        P(),
    )
    return jax.shard_map(
        functools.partial(shards, mesh.shape["tensor"], mesh.shape["section"]),
        mesh=mesh,
        in_specs=placed,
        out_specs=P("section", None, "tensor", None),
        check_vma=False,
    )
```

time: 255 us -> 181 us (0.71)
  waiting for transfers between devices: 188 us -> 0 us
  Pallas kernels: 0 us -> 179 us
  matrix products: 25.1 us -> 0 us
  between operations: 20.1 us -> 0.01 us
  blocking collectives: 13.8 us -> 0 us
  other arithmetic: 5.5 us -> 0 us
    pallas_call x0 -> x1, Pallas kernels: none -> 179 us  [relay_call(): pl.pallas_call(functools.partial(relay_kernel, n, sections, chunks), out_...]
    all_gather x2 -> x0, waiting for transfers between devices: 167 us -> none  [the longest x1 89.4 us: shards(): lax.all_gather(w_out[0], 'tensor', axis=0, tiled=True)]
    dot_general x4 -> x0, matrix products: 25.1 us -> none  [apply_block(): jnp.dot(hidden, full_out, preferred_element_type=jnp.float32)]
    ppermute x4 -> x0, waiting for transfers between devices: 20.2 us -> none  [passed_along(): return lax.ppermute(value, axis, pairs)]
    unnamed x1 -> x0, blocking collectives: 13.8 us -> none
    reduce_sum x8 -> x0, other arithmetic: 4.31 us -> none  [the longest x4 3.44 us: normalize(): average = jnp.mean(widened, axis=-1, keepdims=True)]
  transfers between devices with their start and end apart: 6 -> 0, of which waited for: 6 -> 0; matrix products, arithmetic and copies ran while one was open for 1% -> 0% of each run, Pallas kernels for 0% -> 0%
where the time goes in v1:
time: 181 us
  Pallas kernels  179 us (99%)
  local copies, waits for them, and re-layouts  2.26 us (1%)
    pallas_call x1, Pallas kernels, relay_call(): pl.pallas_call(functools.partial(relay_kernel, n, sections, chunks), out_...  179 us

profile of v1, /device:TPU:0, one launch (start us, length us, event | category | flops | bytes accessed | tf_op | source)
XLA Modules:
  0.0 181.3 jit_solution(12938243555667243810)
XLA Ops:
  0.0 179.0 %shard_map.91 = bf16[16,32,1024]{2,1,0:T(8,128)(2,1)} custom-call(bf16[4,32,1024]{2,1,0:T(8,128)(2,1)} %bitcast.9, bf16[576,1024]{1,0:T(8,128)(2,1)} %bitcast.7, bf16[1,576]{1,0:T(2,128)(2,1)} %ib_ref.1, bf16[576,1024]{1,0:T(8,128)(2,1)} %bitcast.8, f32[1,1024]{1,0:T(1,128)} %ob_ref.1, f32[1,1024]{1,0:T(1,128)} %gain_ref.1, f32[1,1024]{1,0:T(1,128)} %shift_ref.1, ...), custom_call_target="tpu_custom_call" | custom-call | tf_op jit(solution)/shard_map/pallas_call | solution.py:232
  179.0 2.3 %copy.11 = bf16[1,4,128,1024]{3,2,1,0:T(8,128)(2,1)} copy(bf16[1,4,128,1024]{3,2,1,0:T(8,128)(2,1)} %bitcast.5) | data formatting | bytes 2097152

commit v2 on v0

v2 whole, which is shorter than its diff:
```python
import functools

import jax
import jax.numpy as jnp
from jax import lax
from jax.experimental import pallas as pl
from jax.experimental.pallas import tpu as pltpu
from jax.sharding import PartitionSpec as P

TICKS = 4
HOP_SLOTS = 2
VMEM_BYTES = 60 * 1024 * 1024

norm_floor = 0.1
gelu_slope = 1.702
MESH = pl.DeviceIdType.MESH


def activate(preact):
    return preact * jax.nn.sigmoid(gelu_slope * preact)


def normalize(widened, gain_row, shift_row):
    average = jnp.mean(widened, axis=-1, keepdims=True)
    centered = widened - average
    variance = jnp.mean(centered * centered, axis=-1, keepdims=True)
    return (centered * lax.rsqrt(variance + norm_floor) * gain_row + shift_row).astype(
        jnp.bfloat16
    )


def relay_kernel(
    n, sections, hop_slots,
    x_ref, win_ref, ib_ref, wout_ref, ob_ref, gain_ref, shift_ref, patches_ref, plan_ref,
    o_ref,
    held, sums_in, sums_out, staged, total,
    x_send, x_recv, sum_send, sum_recv, ship_send, final_recv,
):
    chunks = n * hop_slots
    items = TICKS * chunks
    pieces = x_ref.shape[0]
    me = lax.axis_index("tensor")
    section = lax.axis_index("section")
    following = lax.rem(section + 1, sections)
    preceding = lax.rem(section + sections - 1, sections)

    barrier = pltpu.get_barrier_semaphore()

    def greet(sect, tensor):
        pl.semaphore_signal(
            barrier, inc=1, device_id={"section": sect, "tensor": tensor}, device_id_type=MESH
        )

    for tensor in range(n):
        greet(following, tensor)
        greet(preceding, tensor)
        pl.when(me != tensor)(functools.partial(greet, section, tensor))
    pl.semaphore_wait(barrier, 3 * n - 1)

    def x_copy(src, group, item, sect, tensor, send_sem):
        return pltpu.make_async_remote_copy(
            src_ref=src,
            dst_ref=held.at[group, item],
            send_sem=send_sem,
            recv_sem=x_recv.at[group, item],
            device_id={"section": sect, "tensor": tensor},
            device_id_type=MESH,
        )

    def forward_copy(group, item, tensor):
        return x_copy(
            held.at[group, item], group, item, section, tensor, x_send.at[group, item]
        )

    def relay_copy(group, item):
        return x_copy(
            sums_out.at[group, item], group, item + chunks, following, me,
            sum_send.at[group, item],
        )

    def sum_copy(group, item, tensor):
        return pltpu.make_async_remote_copy(
            src_ref=sums_out.at[group, item],
            dst_ref=sums_in.at[group, item],
            send_sem=sum_send.at[group, item],
            recv_sem=sum_recv.at[group, item],
            device_id={"section": section, "tensor": tensor},
            device_id_type=MESH,
        )

    def final_copy(group, item, tick, piece, home):
        return pltpu.make_async_remote_copy(
            src_ref=sums_out.at[group, item],
            dst_ref=o_ref.at[tick, piece],
            send_sem=sum_send.at[group, item],
            recv_sem=final_recv.at[tick, piece],
            device_id={"section": following, "tensor": home},
            device_id_type=MESH,
        )

    def place(group, item):
        tick, chunk = lax.div(item, chunks), lax.rem(item, chunks)
        shard, piece = lax.div(chunk, pieces), lax.rem(chunk, pieces)
        home = jnp.where(group == 0, shard, n - 1 - shard)
        right = lax.rem(jnp.minimum(tick, section) + group, 2) == 0
        position = jnp.where(right, me, n - 1 - me)
        target = jnp.where(right, me + 1, me - 1)
        return tick, piece, home, position, target

    my_group = jnp.where(me < n // 2, 0, 1)
    my_start = my_group * (n - 1)
    my_first = jnp.where(me < n // 2, me, n - 1 - me) * pieces

    def enter(tick, piece, carry):
        item = tick * chunks + my_first + piece
        if tick == 0:
            source = x_ref.at[piece]
        else:
            source = staged.at[tick - 1, piece]
            staged[tick - 1, piece] = patches_ref[plan_ref[tick - 1], piece]

        @pl.when(me == my_start)
        def _():
            held[my_group, item] = source[...]

        @pl.when(me != my_start)
        def _():
            x_copy(
                source, my_group, item, section, my_start, ship_send.at[tick, piece]
            ).start()

        return carry

    lax.fori_loop(0, pieces, functools.partial(enter, 0), 0)

    @pl.when(section == 0)
    def _():
        for tick in range(1, TICKS):
            lax.fori_loop(0, pieces, functools.partial(enter, tick), 0)

    def receive(group, item, position):
        tick, piece, home, where, target = place(group, item)

        @pl.when(where == position)
        def _():
            entered = (position == 0) & (home == me) & ((tick == 0) | (section == 0))

            @pl.when(jnp.logical_not(entered))
            def _():
                forward_copy(group, item, target).wait_recv()

            @pl.when(position < n - 1)
            def _():
                forward_copy(group, item, target).start()

            @pl.when((tick > 0) & (section > 0) & (home == me))
            def _():
                o_ref[tick - 1, piece] = held[group, item]

    def compute(group, item, position):
        tick, piece, home, where, target = place(group, item)

        @pl.when(where == position)
        def _():
            normed = normalize(
                held[group, item].astype(jnp.float32), gain_ref[...], shift_ref[...]
            )
            preact = lax.dot_general(
                normed, win_ref[...], (((1,), (1,)), ((), ())),
                preferred_element_type=jnp.float32,
            )
            hidden = activate(preact + ib_ref[...].astype(jnp.float32)).astype(jnp.bfloat16)
            total[...] = jnp.dot(hidden, wout_ref[...], preferred_element_type=jnp.float32)

            @pl.when(position > 0)
            def _():
                sum_copy(group, item, target).wait_recv()
                total[...] += sums_in[group, item].astype(jnp.float32)

            @pl.when(position < n - 1)
            def _():
                sums_out[group, item] = total[...].astype(jnp.bfloat16)
                sum_copy(group, item, target).start()

            @pl.when(position == n - 1)
            def _():
                sums_out[group, item] = (
                    held[group, item].astype(jnp.float32) + total[...] + ob_ref[...]
                ).astype(jnp.bfloat16)
                leaves = (tick == TICKS - 1) | (following == 0)

                @pl.when(leaves)
                def _():
                    final_copy(group, item, tick, piece, home).start()

                @pl.when(jnp.logical_not(leaves))
                def _():
                    relay_copy(group, item).start()

    def each(action, slot):
        def one(index, carry):
            group, position = lax.rem(index, 2), n - 1 - lax.div(index, 2)
            item = slot - position * hop_slots
            pl.when((item >= 0) & (item < items))(
                functools.partial(action, group, item, position)
            )
            return carry

        lax.fori_loop(0, 2 * n, one, 0)

    def turn(slot, carry):
        each(receive, slot)
        each(compute, slot)
        return carry

    lax.fori_loop(0, items + (n - 1) * hop_slots, turn, 0)

    def drain(item, carry):
        for group in range(2):
            tick, piece, home, position, target = place(group, item)

            @pl.when(position < n - 1)
            def _():
                forward_copy(group, item, target).wait_send()

            sum_copy(group, item, target).wait_send()

            @pl.when((home == me) & ((tick == TICKS - 1) | (section == 0)))
            def _():
                final_copy(group, item, tick, piece, home).wait_recv()

            sent = (home == me) & (me != my_start) & ((tick == 0) | (section == 0))

            @pl.when(sent)
            def _():
                x_copy(
                    staged.at[0, piece], group, item, section, my_start,
                    ship_send.at[tick, piece],
                ).wait_send()

        return carry

    lax.fori_loop(0, items, drain, 0)


def relay_call(n, sections, hop_slots, args):
    x, w_in, in_bias, w_out, out_bias, gain, shift, patches, plan = args
    tokens, width = x.shape
    pieces = 2 * hop_slots
    rows = tokens // pieces
    items = TICKS * n * hop_slots
    micro = patches.shape[0]
    bf16 = jnp.bfloat16
    vmem = pl.BlockSpec(memory_space=pltpu.VMEM)
    every = (2, items, rows, width)
    dma = pltpu.SemaphoreType.DMA
    out = pl.pallas_call(
        functools.partial(relay_kernel, n, sections, hop_slots),
        out_shape=jax.ShapeDtypeStruct((TICKS, pieces, rows, width), bf16),
        in_specs=[vmem] * 8 + [pl.BlockSpec(memory_space=pltpu.SMEM)],
        out_specs=vmem,
        scratch_shapes=[
            pltpu.VMEM(every, bf16),
            pltpu.VMEM(every, bf16),
            pltpu.VMEM(every, bf16),
            pltpu.VMEM((TICKS - 1, pieces, rows, width), bf16),
            pltpu.VMEM((rows, width), jnp.float32),
            dma((2, items)),
            dma((2, items)),
            dma((2, items)),
            dma((2, items)),
            dma((TICKS, pieces)),
            dma((TICKS, pieces)),
        ],
        compiler_params=pltpu.CompilerParams(
            collective_id=0, has_side_effects=True, vmem_limit_bytes=VMEM_BYTES
        ),
    )(
        x.reshape(pieces, rows, width),
        w_in,
        in_bias.reshape(1, -1),
        w_out,
        out_bias.reshape(1, -1),
        gain.reshape(1, -1),
        shift.reshape(1, -1),
        patches.reshape(micro, pieces, rows, width),
        plan,
    )
    return out.reshape(1, TICKS, tokens, width)


def passed_along(value, axis, steps):
    count = lax.axis_size(axis)
    pairs = [(source, (source + steps) % count) for source in range(count)]
    return lax.ppermute(value, axis, pairs)


def gathered_weights(args):
    current, w_in, in_bias, w_out, bias_row, gain_row, shift_row, patches, plan = args
    section_index = lax.axis_index("section")
    full_in, full_bias, full_out = (
        lax.all_gather(value, "tensor", axis=0, tiled=True) for value in (w_in, in_bias, w_out)
    )
    records = []
    for tick_index in range(TICKS):
        widened = current.astype(jnp.float32)
        normed = normalize(widened, gain_row, shift_row)
        preact = lax.dot_general(
            normed, full_in, (((1,), (1,)), ((), ())), preferred_element_type=jnp.float32
        )
        hidden = activate(preact + full_bias.astype(jnp.float32)).astype(jnp.bfloat16)
        produced = (
            widened + jnp.dot(hidden, full_out, preferred_element_type=jnp.float32) + bias_row
        ).astype(jnp.bfloat16)
        arrived = passed_along(produced, "section", 1)
        records.append(arrived)
        if tick_index + 1 < TICKS:
            selected = lax.dynamic_index_in_dim(patches, plan[tick_index], 0, keepdims=False)
            current = jnp.where(section_index == 0, selected, arrived)
    return jnp.stack(records, axis=0)[None]


def shards(n, sections, *blocks):
    args = tuple(block[0] for block in blocks[:7]) + blocks[7:]
    tokens, width = args[0].shape
    room = 2 * width * (
        tokens * (TICKS * (3 * n + 2) + 1 + args[7].shape[0]) + 2 * args[1].shape[0]
    )
    if tokens % (HOP_SLOTS * 32) or n % 2 or sections < 2 or room > VMEM_BYTES * 3 // 4:
        return gathered_weights(args)
    return relay_call(n, sections, HOP_SLOTS, args)


def solution(mesh):
    placed = (
        P("section", "tensor", None),
        P("section", "tensor", None),
        P("section", "tensor"),
        P("section", "tensor", None),
        P("section", None),
        P("section", None),
        P("section", None),
        P(None, "tensor", None),
        P(),
    )
    return jax.shard_map(
        functools.partial(shards, mesh.shape["tensor"], mesh.shape["section"]),
        mesh=mesh,
        in_specs=placed,
        out_specs=P("section", None, "tensor", None),
        check_vma=False,
    )
```

time: 255 us -> 132 us (0.52)
  the two profiles are of different devices: /device:TPU:0 before, /device:TPU:8 now
where the time goes in v2:
time: 132 us
  Pallas kernels  130 us (98%)
  local copies, waits for them, and re-layouts  2.26 us (2%)
    pallas_call x1, Pallas kernels, relay_call(): pl.pallas_call(functools.partial(relay_kernel, n, sections, hop_slots), o...  130 us

profile of v2, /device:TPU:8, one launch (start us, length us, event | category | flops | bytes accessed | tf_op | source)
XLA Modules:
  0.0 131.9 jit_solution(5799274284844318422)
XLA Ops:
  0.0 129.7 %shard_map.91 = bf16[4,4,32,1024]{3,2,1,0:T(8,128)(2,1)} custom-call(bf16[4,32,1024]{2,1,0:T(8,128)(2,1)} %bitcast.9, bf16[576,1024]{1,0:T(8,128)(2,1)} %bitcast.7, bf16[1,576]{1,0:T(2,128)(2,1)} %ib_ref.1, bf16[576,1024]{1,0:T(8,128)(2,1)} %bitcast.8, f32[1,1024]{1,0:T(1,128)} %ob_ref.1, f32[1,1024]{1,0:T(1,128)} %gain_ref.1, f32[1,1024]{1,0:T(1,128)} %shift_ref.1, ...), custom_call_target="tpu_custom_call" | custom-call | tf_op jit(solution)/shard_map/pallas_call | solution.py:257
  129.7 2.3 %copy.11 = bf16[1,4,128,1024]{3,2,1,0:T(8,128)(2,1)} copy(bf16[1,4,128,1024]{3,2,1,0:T(8,128)(2,1)} %bitcast.5) | data formatting | bytes 2097152

commit v3 on v2

--- a/solution.py
+++ b/solution.py
@@ -8,6 +8,7 @@
 from jax.sharding import PartitionSpec as P
 
 TICKS = 4
+PIECES = 4
 HOP_SLOTS = 2
 VMEM_BYTES = 60 * 1024 * 1024
 
@@ -31,18 +32,28 @@
 
 def relay_kernel(
     n, sections, hop_slots,
-    x_ref, win_ref, ib_ref, wout_ref, ob_ref, gain_ref, shift_ref, patches_ref, plan_ref,
+    x_ref, win_hbm, ib_ref, wout_hbm, ob_ref, gain_ref, shift_ref, patches_hbm, plan_ref,
     o_ref,
-    held, sums_in, sums_out, staged, total,
+    win_ref, wout_ref, patches_ref, load_sem, held, sums_in, sums_out, staged, total,
     x_send, x_recv, sum_send, sum_recv, ship_send, final_recv,
 ):
-    chunks = n * hop_slots
+    pieces = x_ref.shape[0]
+    chunks = n // 2 * pieces
     items = TICKS * chunks
-    pieces = x_ref.shape[0]
     me = lax.axis_index("tensor")
     section = lax.axis_index("section")
     following = lax.rem(section + 1, sections)
     preceding = lax.rem(section + sections - 1, sections)
+
+    loads = [
+        pltpu.make_async_copy(source, target, load_sem.at[index])
+        for index, (source, target) in enumerate(
+            [(win_hbm, win_ref), (wout_hbm, wout_ref), (patches_hbm, patches_ref)]
+        )
+    ]
+    for load in loads[:2]:
+        load.start()
+    pl.when(section == 0)(loads[2].start)
 
     barrier = pltpu.get_barrier_semaphore()
 
@@ -98,35 +109,41 @@
             device_id_type=MESH,
         )
 
+    def entry_side(origin):
+        later = sections - 1 - origin
+        far = (origin >= 0) & (later < TICKS) & (lax.rem(later, 2) == 0)
+        return far.astype(jnp.int32)
+
     def place(group, item):
         tick, chunk = lax.div(item, chunks), lax.rem(item, chunks)
         shard, piece = lax.div(chunk, pieces), lax.rem(chunk, pieces)
         home = jnp.where(group == 0, shard, n - 1 - shard)
-        right = lax.rem(jnp.minimum(tick, section) + group, 2) == 0
+        turns = jnp.minimum(tick, section) + entry_side(section - tick) + group
+        right = lax.rem(turns, 2) == 0
         position = jnp.where(right, me, n - 1 - me)
         target = jnp.where(right, me + 1, me - 1)
         return tick, piece, home, position, target
 
     my_group = jnp.where(me < n // 2, 0, 1)
-    my_start = my_group * (n - 1)
+    my_start = lax.rem(my_group + entry_side(section), 2) * (n - 1)
+    my_side = my_group * (n - 1)
     my_first = jnp.where(me < n // 2, me, n - 1 - me) * pieces
 
     def enter(tick, piece, carry):
         item = tick * chunks + my_first + piece
         if tick == 0:
-            source = x_ref.at[piece]
+            source, start = x_ref.at[piece], my_start
         else:
+            start = my_side
             source = staged.at[tick - 1, piece]
             staged[tick - 1, piece] = patches_ref[plan_ref[tick - 1], piece]
 
-        @pl.when(me == my_start)
-        def _():
-            held[my_group, item] = source[...]
-
-        @pl.when(me != my_start)
+        held[my_group, item] = source[...]
+
+        @pl.when(me != start)
         def _():
             x_copy(
-                source, my_group, item, section, my_start, ship_send.at[tick, piece]
+                source, my_group, item, section, start, ship_send.at[tick, piece]
             ).start()
 
         return carry
@@ -135,21 +152,25 @@
 
     @pl.when(section == 0)
     def _():
+        loads[2].wait()
         for tick in range(1, TICKS):
             lax.fori_loop(0, pieces, functools.partial(enter, tick), 0)
 
+    for load in loads[:2]:
+        load.wait()
+
     def receive(group, item, position):
         tick, piece, home, where, target = place(group, item)
 
         @pl.when(where == position)
         def _():
-            entered = (position == 0) & (home == me) & ((tick == 0) | (section == 0))
-
-            @pl.when(jnp.logical_not(entered))
+            entry = (tick == 0) | (section == 0)
+
+            @pl.when(jnp.logical_not(entry & (home == me)))
             def _():
                 forward_copy(group, item, target).wait_recv()
 
-            @pl.when(position < n - 1)
+            @pl.when((position < n - 1) & jnp.logical_not(entry & (home == target)))
             def _():
                 forward_copy(group, item, target).start()
 
@@ -219,7 +240,9 @@
         for group in range(2):
             tick, piece, home, position, target = place(group, item)
 
-            @pl.when(position < n - 1)
+            entry = (tick == 0) | (section == 0)
+
+            @pl.when((position < n - 1) & jnp.logical_not(entry & (home == target)))
             def _():
                 forward_copy(group, item, target).wait_send()
 
@@ -229,12 +252,13 @@
             def _():
                 final_copy(group, item, tick, piece, home).wait_recv()
 
-            sent = (home == me) & (me != my_start) & ((tick == 0) | (section == 0))
+            start = jnp.where(tick == 0, my_start, my_side)
+            sent = (home == me) & (me != start) & entry
 
             @pl.when(sent)
             def _():
                 x_copy(
-                    staged.at[0, piece], group, item, section, my_start,
+                    staged.at[0, piece], group, item, section, start,
                     ship_send.at[tick, piece],
                 ).wait_send()
 
@@ -243,23 +267,28 @@
     lax.fori_loop(0, items, drain, 0)
 
 
-def relay_call(n, sections, hop_slots, args):
+def relay_call(n, sections, pieces, hop_slots, args):
     x, w_in, in_bias, w_out, out_bias, gain, shift, patches, plan = args
     tokens, width = x.shape
-    pieces = 2 * hop_slots
     rows = tokens // pieces
-    items = TICKS * n * hop_slots
+    items = TICKS * n // 2 * pieces
     micro = patches.shape[0]
     bf16 = jnp.bfloat16
     vmem = pl.BlockSpec(memory_space=pltpu.VMEM)
+    hbm = pl.BlockSpec(memory_space=pl.ANY)
     every = (2, items, rows, width)
     dma = pltpu.SemaphoreType.DMA
     out = pl.pallas_call(
         functools.partial(relay_kernel, n, sections, hop_slots),
         out_shape=jax.ShapeDtypeStruct((TICKS, pieces, rows, width), bf16),
-        in_specs=[vmem] * 8 + [pl.BlockSpec(memory_space=pltpu.SMEM)],
+        in_specs=[vmem, hbm, vmem, hbm, vmem, vmem, vmem, hbm]
+        + [pl.BlockSpec(memory_space=pltpu.SMEM)],
         out_specs=vmem,
         scratch_shapes=[
+            pltpu.VMEM(w_in.shape, bf16),
+            pltpu.VMEM(w_out.shape, bf16),
+            pltpu.VMEM((micro, pieces, rows, width), bf16),
+            dma((3,)),
             pltpu.VMEM(every, bf16),
             pltpu.VMEM(every, bf16),
             pltpu.VMEM(every, bf16),
@@ -326,9 +355,9 @@
     room = 2 * width * (
         tokens * (TICKS * (3 * n + 2) + 1 + args[7].shape[0]) + 2 * args[1].shape[0]
     )
-    if tokens % (HOP_SLOTS * 32) or n % 2 or sections < 2 or room > VMEM_BYTES * 3 // 4:
+    if tokens % (PIECES * 16) or n % 2 or sections < 2 or room > VMEM_BYTES * 3 // 4:
         return gathered_weights(args)
-    return relay_call(n, sections, HOP_SLOTS, args)
+    return relay_call(n, sections, PIECES, HOP_SLOTS, args)
 
 
 def solution(mesh):

time: 132 us -> 124 us (0.939)
  the two profiles are of different devices: /device:TPU:8 before, /device:TPU:0 now
where the time goes in v3:
time: 124 us; the launch traced here: 123 us
  Pallas kernels  121 us (98%)
  local copies, waits for them, and re-layouts  2.26 us (2%)
    pallas_call x1, Pallas kernels, relay_call(): pl.pallas_call(functools.partial(relay_kernel, n, sections, hop_slots), o...  121 us

profile of v3, /device:TPU:0, one launch (start us, length us, event | category | flops | bytes accessed | tf_op | source)
XLA Modules:
  0.0 123.3 jit_solution(9593323250159538989)
XLA Ops:
  0.0 121.0 %shard_map.91 = bf16[4,4,32,1024]{3,2,1,0:T(8,128)(2,1)} custom-call(bf16[4,32,1024]{2,1,0:T(8,128)(2,1)} %bitcast.9, bf16[576,1024]{1,0:T(8,128)(2,1)} %bitcast.7, bf16[1,576]{1,0:T(2,128)(2,1)} %ib_ref.1, bf16[576,1024]{1,0:T(8,128)(2,1)} %bitcast.8, f32[1,1024]{1,0:T(1,128)} %ob_ref.1, f32[1,1024]{1,0:T(1,128)} %gain_ref.1, f32[1,1024]{1,0:T(1,128)} %shift_ref.1, ...), custom_call_target="tpu_custom_call" | custom-call | tf_op jit(solution)/shard_map/pallas_call | solution.py:281
  121.1 2.3 %copy.11 = bf16[1,4,128,1024]{3,2,1,0:T(8,128)(2,1)} copy(bf16[1,4,128,1024]{3,2,1,0:T(8,128)(2,1)} %bitcast.5) | data formatting | bytes 2097152

commit v4 on v3

--- a/solution.py
+++ b/solution.py
@@ -156,9 +156,6 @@
         for tick in range(1, TICKS):
             lax.fori_loop(0, pieces, functools.partial(enter, tick), 0)
 
-    for load in loads[:2]:
-        load.wait()
-
     def receive(group, item, position):
         tick, piece, home, where, target = place(group, item)
 
@@ -220,7 +217,7 @@
 
     def each(action, slot):
         def one(index, carry):
-            group, position = lax.rem(index, 2), n - 1 - lax.div(index, 2)
+            group, position = lax.rem(index, 2), lax.div(index, 2)
             item = slot - position * hop_slots
             pl.when((item >= 0) & (item < items))(
                 functools.partial(action, group, item, position)
@@ -230,10 +227,13 @@
         lax.fori_loop(0, 2 * n, one, 0)
 
     def turn(slot, carry):
-        each(receive, slot)
         each(compute, slot)
+        each(receive, slot + 1)
         return carry
 
+    each(receive, 0)
+    for load in loads[:2]:
+        load.wait()
     lax.fori_loop(0, items + (n - 1) * hop_slots, turn, 0)
 
     def drain(item, carry):

time: 124 us -> 123 us (level)
  no operation moved by 1% of the time
where the time goes in v4:
time: 123 us
  Pallas kernels  121 us (98%)
  local copies, waits for them, and re-layouts  2.26 us (2%)
    pallas_call x1, Pallas kernels, relay_call(): pl.pallas_call(functools.partial(relay_kernel, n, sections, hop_slots), o...  121 us

profile of v4, /device:TPU:0, one launch (start us, length us, event | category | flops | bytes accessed | tf_op | source)
XLA Modules:
  0.0 123.3 jit_solution(7348716928373447908)
XLA Ops:
  0.0 121.0 %shard_map.91 = bf16[4,4,32,1024]{3,2,1,0:T(8,128)(2,1)} custom-call(bf16[4,32,1024]{2,1,0:T(8,128)(2,1)} %bitcast.9, bf16[576,1024]{1,0:T(8,128)(2,1)} %bitcast.7, bf16[1,576]{1,0:T(2,128)(2,1)} %ib_ref.1, bf16[576,1024]{1,0:T(8,128)(2,1)} %bitcast.8, f32[1,1024]{1,0:T(1,128)} %ob_ref.1, f32[1,1024]{1,0:T(1,128)} %gain_ref.1, f32[1,1024]{1,0:T(1,128)} %shift_ref.1, ...), custom_call_target="tpu_custom_call" | custom-call | tf_op jit(solution)/shard_map/pallas_call | solution.py:281
  121.1 2.3 %copy.11 = bf16[1,4,128,1024]{3,2,1,0:T(8,128)(2,1)} copy(bf16[1,4,128,1024]{3,2,1,0:T(8,128)(2,1)} %bitcast.5) | data formatting | bytes 2097152
